TPU v7x, 128 devices: a whole 4x4x4 slice. The times are simulated.
128 devices in a mesh: seg: 32 (over y_lo, x, z), rep: 4 (over y_hi, core).
Axes of the slice: x: 4, y: 4 (y_hi: 2, y_lo: 2; y = y_hi * 2 + y_lo), z: 4, core: 2. Of those that a mesh axis runs over, the one named last changes fastest.
Arguments:
- decoder_rows: bfloat16 [256, 4096], P('rep', 'seg'), may hold values from -2000 to 2000
- norm_gain: float32 [4096], replicated, may hold values from 0.5 to 1.5
- query_weight: bfloat16 [4096, 4096], P('rep', 'seg'), may hold values from -1 to 1
- key_codes: bfloat16 [4, 16384, 4096], P('rep', 'seg'), may hold values from -127 to 127, as said below
- key_scale: float32 [4, 128, 64], P('rep', 'seg'), may hold values from 0.5 to 1.5
- value_codes: bfloat16 [4, 16384, 4096], P('rep', 'seg'), may hold values from -6 to 6
- value_scale: float32 [4, 128, 64], P('rep', 'seg'), may hold values from 0.5 to 2
- enc_lengths: int32 [4], P('rep'), may hold values from 4096 to 16384
- output_weight: bfloat16 [4096, 4096], P('seg', 'rep'), may hold values from -0.09375 to 0.09375
Outputs:
- update: bfloat16 [256, 4096], P('rep', 'seg')
Inputs may be any that keep to these rules, and one draw needn't show every extreme that they name: `key_codes`: codes of a block times its scale give the cached keys.
All inputs are finite; a program needn't handle non-finite values.
Results may differ from a plain program's by a relative error of at most 0.011.
Values may be sent and summed in bfloat16 or wider, within the bound.
No kernel may reach another device: no remote copies, remote signals or barrier semaphores. Data moves between devices by JAX's collectives and lax.ppermute only.
A program may use at most 64 MiB of HBM per device.

v0:
```python
import math

import jax
import jax.numpy as jnp
from jax import lax
from jax.experimental import pallas as pl
from jax.experimental.pallas import tpu as pltpu
from jax.sharding import PartitionSpec as P

LOG2E = math.log2(math.e)
BF16, F32 = jnp.bfloat16, jnp.float32
LANES = 128
STAT_ROWS = 8
SUM_ROWS = 16
EMPTY = -1e30
FIRST = 10
LAST = 26
VMEM = pl.BlockSpec(memory_space=pltpu.VMEM)
SMEM = pl.BlockSpec(memory_space=pltpu.SMEM)
HBM = pl.BlockSpec(memory_space=pltpu.HBM)


def params(mib):
    return pltpu.CompilerParams(vmem_limit_bytes=mib << 20)


def cost(flops, moved):
    return pl.CostEstimate(flops=flops, bytes_accessed=moved, transcendentals=0)


def flip_pair(block):
    half = block.shape[0]
    turned = jnp.concatenate([block, block], axis=0).T
    left = lax.broadcasted_iota(jnp.int32, block.shape, 1) < half
    return jnp.where(left, turned[:half], turned[half:])


def query_kernel(rep_ref, x_ref, gain_ref, *refs):
    weights, out_ref = refs[:-1], refs[-1]
    segs, rows, _ = x_ref.shape
    squares = jnp.zeros((rows, LANES), F32)
    for j in range(segs):
        wide = x_ref[j].astype(F32)
        squares += wide * wide
    mean = jnp.sum(squares, axis=1, keepdims=True) * (1.0 / (segs * LANES))
    scale = lax.rsqrt(mean + 1e-06)
    each = segs // len(weights)
    total = jnp.zeros((rows, LANES), F32)
    for i, w_ref in enumerate(weights):
        first = (rep_ref[0] ^ i) * each
        for j in range(0, each, 2):
            pair = [
                (x_ref[(first + k) ^ FIRST].astype(F32) * scale * gain_ref[pl.ds(first + k, 1), :]).astype(BF16)
                for k in (j, j + 1)
            ]
            total += jnp.dot(
                jnp.concatenate(pair, axis=1),
                w_ref[j * LANES : (j + 2) * LANES, :],
                preferred_element_type=F32,
            )
    own = flip_pair(total).astype(BF16)
    for j in range(segs):
        out_ref[j] = own


def stage_kernel(own_ref, gain_ref, own_out, gain_out):
    own_out[...] = own_ref[...]
    gain_out[...] = gain_ref[...]


def picks_of(tokens):
    row = lax.broadcasted_iota(jnp.int32, (SUM_ROWS, tokens), 0)
    block = lax.broadcasted_iota(jnp.int32, (SUM_ROWS, tokens), 1) // LANES
    return jnp.where(row == block, 1.0, 0.0).astype(BF16)


def turn_kernel(v_ref, k_ref, out_ref, k_first, vt_first):
    for j in range(out_ref.shape[0]):
        for i in range(2):
            at = slice((2 * j + i) * LANES, (2 * j + i + 1) * LANES)
            out_ref[j, i] = v_ref[:, at].T

    @pl.when(pl.program_id(0) == 0)
    def _():
        for g in range(k_first.shape[0]):
            k_first[g] = k_ref[:, 2 * g * LANES : 2 * (g + 1) * LANES]
        picks = picks_of(v_ref.shape[0])
        for j in range(vt_first.shape[0]):
            for i in range(2):
                vt_first[j, i, 0:LANES, :] = out_ref[j, i]
                vt_first[j, i, LANES : LANES + SUM_ROWS, :] = picks


def attend_kernel(
    used_ref, q_ref, ks_ref, lvs_ref, ivs_ref, k_first, vt_first, k_hbm, vt_hbm, out_hbm,
    out_ref, k_buf, vt_buf, s0, s1, p0, p1, m0, m1, n0, n1, k_sems, vt_sems, out_sems,
):
    groups = vt_hbm.shape[0]
    half = q_ref.shape[1]
    blocks = ks_ref.shape[0]
    wide = 2 * LANES
    used = used_ref[0]
    sub = lax.broadcasted_iota(jnp.int32, (STAT_ROWS, LANES), 0)
    left = lax.broadcasted_iota(jnp.int32, (half, LANES), 1) < half

    def lanes_of(g):
        return pl.ds(g * wide if isinstance(g, int) else pl.multiple_of(g * wide, wide), wide)

    def k_copy(g):
        return pltpu.make_async_copy(k_hbm.at[:, lanes_of(g)], k_buf.at[g], k_sems.at[g])

    def vt_copy(g):
        return pltpu.make_async_copy(
            vt_hbm.at[g], vt_buf.at[g, :, pl.ds(0, LANES), :], vt_sems.at[g]
        )

    def out_copy(g):
        at = pl.ds((2 * g) ^ FIRST, 2)
        return pltpu.make_async_copy(out_ref.at[at], out_hbm.at[at], out_sems.at[g])

    k_early, vt_early = k_first.shape[0], vt_first.shape[0]

    def fetch(i):
        for g in (2 * i, 2 * i + 1):
            if not isinstance(i, int) or g < groups:
                k_copy(g).start()
            vt_copy(g - 2).start()

    for i in range(2, groups // 2 + 1):
        fetch(i)

    picks = picks_of(k_buf.shape[1])
    for g in range(vt_early, groups):
        for i in range(2):
            vt_buf[g, i, LANES : LANES + SUM_ROWS, :] = picks

    def put(pair, sums, log_sum):
        out_ref[pair ^ FIRST, 0:half, :] = sums.astype(BF16)
        high = log_sum.astype(BF16).astype(F32)
        mid = (log_sum - high).astype(BF16).astype(F32)
        low = log_sum - high - mid
        stats = jnp.where(sub == 0, high, jnp.where(sub == 1, mid, jnp.where(sub == 2, low, 0.0)))
        out_ref[pair ^ FIRST, half : half + STAT_ROWS, :] = stats.astype(BF16)

    def rows_of(b):
        return slice(b * LANES, (b + 1) * LANES)

    def score(g, count, clear, s_ref, m_ref):
        none = jnp.zeros((half, LANES), BF16)
        q0, q1 = q_ref[(2 * g) ^ FIRST], q_ref[(2 * g + 1) ^ FIRST]
        placed = jnp.concatenate(
            [
                jnp.concatenate([jnp.where(left, q0, none), none], axis=1),
                jnp.concatenate([jnp.where(left, none, q0), none], axis=1),
                jnp.concatenate([none, jnp.where(left, q1, none)], axis=1),
                jnp.concatenate([none, jnp.where(left, none, q1)], axis=1),
            ],
            axis=0,
        )
        peak = None
        keys = k_first if isinstance(g, int) and g < k_early else k_buf
        for b in range(count):
            part = jnp.dot(keys[g, rows_of(b), :], placed, preferred_element_type=F32)
            part = part * ks_ref[b : b + 1, lanes_of(g)]
            if b >= clear:
                place = b * LANES + lax.broadcasted_iota(jnp.int32, part.shape, 0)
                part = jnp.where(place < used, part, EMPTY)
            s_ref[rows_of(b), :] = part
            top = jnp.max(part, axis=0, keepdims=True)
            peak = top if peak is None else jnp.maximum(peak, top)
            yield
        m_ref[...] = peak

    def weigh(g, count, s_ref, m_ref, p_ref, n_ref):
        peak = m_ref[...]
        n_ref[...] = peak
        for b in range(count):
            shift = peak - lvs_ref[b : b + 1, lanes_of(g)]
            p_ref[rows_of(b), :] = jnp.exp2(s_ref[rows_of(b), :] - shift).astype(BF16)
            yield

    def gather(g, count, p_ref, n_ref):
        inverse_scale = ivs_ref[:, lanes_of(g)]
        for i in range(2):
            at = rows_of(i)
            values = vt_first if isinstance(g, int) and g < vt_early else vt_buf
            sums = jnp.dot(
                values[g, i, :, 0 : count * LANES],
                p_ref[0 : count * LANES, at],
                preferred_element_type=F32,
            )
            yield
            total = jnp.sum(
                sums[LANES : LANES + count] * inverse_scale[0:count, at], axis=0, keepdims=True
            )
            mine = jnp.where(left, sums[0:half], sums[half:LANES])
            put(2 * g + i, mine * (1.0 / total), n_ref[:, at] + jnp.log2(total))
            yield

    def together(*stages):
        stages = list(stages)
        while stages:
            for stage in list(stages):
                if next(stage, stage) is stage:
                    stages.remove(stage)

    def run(count, clear):
        together(score(0, count, clear, s0, m0))
        together(score(1, count, clear, s1, m1), weigh(0, count, s0, m0, p0, n0))

        def two(i):
            together(
                gather(2 * i - 2, count, p0, n0),
                score(2 * i, count, clear, s0, m0),
                weigh(2 * i - 1, count, s1, m1, p1, n1),
            )
            together(
                gather(2 * i - 1, count, p1, n1),
                score(2 * i + 1, count, clear, s1, m1),
                weigh(2 * i, count, s0, m0, p0, n0),
            )

        def more(i, carry):
            for g in (2 * i, 2 * i + 1):
                k_copy(g).wait()
                vt_copy(g - 2).wait()
                out_copy(g - 4).start()

            two(i)
            return carry

        steps = groups // 2
        two(1)
        lax.fori_loop(2, steps, more, 0)
        out_copy(groups - 4).start()
        out_copy(groups - 3).start()
        vt_copy(groups - 2).wait()
        vt_copy(groups - 1).wait()
        together(gather(groups - 2, count, p0, n0), weigh(groups - 1, count, s1, m1, p1, n1))
        out_copy(groups - 2).start()
        together(gather(groups - 1, count, p1, n1))
        out_copy(groups - 1).start()
        for g in range(groups):
            out_copy(g).wait()

    most = (blocks - 1) * LANES

    @pl.when(used <= 0)
    def _():
        for pair in range(2 * groups):
            put(pair, jnp.zeros((half, LANES), F32), jnp.full((1, LANES), EMPTY, F32))
        for g in range(groups):
            out_copy(g).start()
        for g in range(4, groups + 2):
            if g < groups:
                k_copy(g).wait()
            vt_copy(g - 2).wait()
        for g in range(groups):
            out_copy(g).wait()

    @pl.when((used > 0) & (used <= most))
    def _():
        run(blocks - 1, 0)

    @pl.when(used > most)
    def _():
        run(blocks, blocks - 1)


def output_kernel(rep_ref, part_ref, *refs):
    weights, out_ref = refs[:-1], refs[-1]
    segs = part_ref.shape[0]
    half = part_ref.shape[1] - STAT_ROWS
    log_sum = jnp.sum(part_ref[:, half : half + STAT_ROWS, :].astype(F32), axis=1)
    share = jnp.exp2(log_sum - jnp.max(log_sum, axis=0, keepdims=True))
    share = share / jnp.sum(share, axis=0, keepdims=True)
    total = jnp.zeros((half, LANES), F32)
    for j in range(segs):
        total += part_ref[j, 0:half, :].astype(F32) * share[j : j + 1, :]
    attended = flip_pair(total).astype(BF16)
    each = segs // len(weights)
    for i, w_ref in enumerate(weights):
        first = (rep_ref[0] ^ i) * each
        update = jnp.dot(attended, w_ref[...], preferred_element_type=F32)
        for j in range(each):
            out_ref[(first + j) ^ LAST] = update[:, j * LANES : (j + 1) * LANES].astype(BF16)


def sum_kernel(part_ref, out_ref):
    total = part_ref[0].astype(F32)
    for j in range(1, part_ref.shape[0]):
        total += part_ref[j].astype(F32)
    out_ref[...] = total.astype(BF16)


CORE = [(0, 1), (1, 0), (2, 3), (3, 2)]
CHIP = [(0, 2), (1, 3), (2, 0), (3, 1)]


def over_rep(block):
    far = lax.ppermute(block, "rep", CHIP)
    near = lax.ppermute(block, "rep", CORE)
    both = lax.ppermute(far, "rep", CORE)
    return block, near, far, both


def swapped(blocks, lead=FIRST):
    order = [[j ^ lead for j in range(blocks.shape[0])]]
    return lax.all_to_all(
        blocks, "seg", split_axis=0, concat_axis=0, tiled=True, axis_index_groups=order
    )


def sublayer(
    decoder_rows,
    norm_gain,
    query_weight,
    key_codes,
    key_scale,
    value_codes,
    value_scale,
    enc_lengths,
    output_weight,
):
    segs = lax.axis_size("seg")
    rows, own = decoder_rows.shape
    _, tokens, inner = key_codes.shape
    _, heads = key_scale.shape[1:]
    head_dim = inner // heads
    rep = lax.axis_index("rep").astype(jnp.int32).reshape(1)
    used = jnp.clip(enc_lengths - lax.axis_index("seg") * tokens, 0, tokens).astype(jnp.int32)
    gain = norm_gain.reshape(segs, own)
    key_lanes = jnp.repeat(key_scale[0] * LOG2E, head_dim, axis=1)
    value_logs = jnp.repeat(jnp.log2(value_scale[0]), head_dim, axis=1)
    value_inverse = jnp.repeat(1.0 / value_scale[0], head_dim, axis=1)

    wq, wq_near, wq_far, wq_both = over_rep(query_weight)
    x_all = swapped(jnp.broadcast_to(decoder_rows[None], (segs, rows, own)))
    groups, wide = inner // (2 * LANES), 2 * LANES
    height = LANES + SUM_ROWS
    steps = 4
    turn_call = pl.pallas_call(
        turn_kernel,
        grid=(steps,),
        out_shape=(
            jax.ShapeDtypeStruct((groups, 2, LANES, tokens), BF16),
            jax.ShapeDtypeStruct((4, tokens, wide), BF16),
            jax.ShapeDtypeStruct((2, 2, height, tokens), BF16),
        ),
        in_specs=[
            pl.BlockSpec((tokens, inner // steps), lambda i: (0, i)),
            pl.BlockSpec((tokens, 4 * wide), lambda i: (0, 0)),
        ],
        out_specs=(
            pl.BlockSpec((groups // steps, 2, LANES, tokens), lambda i: (i, 0, 0, 0)),
            pl.BlockSpec((4, tokens, wide), lambda i: (0, 0, 0)),
            pl.BlockSpec((2, 2, height, tokens), lambda i: (0, 0, 0, 0)),
        ),
        compiler_params=params(51),
        cost_estimate=cost(2 * inner * tokens * 512, 8 << 20),
        name="turn",
    )
    values_t, first_keys, first_values = turn_call(value_codes[0], key_codes[0])

    stage_call = pl.pallas_call(
        stage_kernel,
        out_shape=(
            jax.ShapeDtypeStruct(wq.shape, BF16),
            jax.ShapeDtypeStruct(gain.shape, F32),
        ),
        in_specs=[VMEM] * 2,
        out_specs=(VMEM, VMEM),
        compiler_params=params(8),
        cost_estimate=cost(1 << 24, 1 << 20),
        name="stage",
    )
    wq, gain = stage_call(wq, gain)
    query_call = pl.pallas_call(
        query_kernel,
        out_shape=jax.ShapeDtypeStruct((segs, head_dim, LANES), BF16),
        in_specs=[SMEM] + [VMEM] * 6,
        out_specs=VMEM,
        compiler_params=params(16),
        cost_estimate=cost(2 * rows * inner * own, 2 << 20),
        name="query",
    )
    x_all, key_lanes, value_logs, value_inverse = lax.optimization_barrier(
        (x_all, key_lanes, value_logs, value_inverse)
    )
    query_sent = query_call(rep, x_all, gain, wq, wq_near, wq_far, wq_both)
    queries = swapped(query_sent)

    parts = pl.pallas_call(
        attend_kernel,
        out_shape=jax.ShapeDtypeStruct((segs, head_dim + STAT_ROWS, LANES), BF16),
        in_specs=[SMEM] + [VMEM] * 6 + [HBM] * 2,
        out_specs=HBM,
        scratch_shapes=[
            pltpu.VMEM((segs, head_dim + STAT_ROWS, LANES), BF16),
            pltpu.VMEM((groups, tokens, wide), BF16),
            pltpu.VMEM((groups, 2, height, tokens), BF16),
        ]
        + [pltpu.VMEM((tokens, wide), F32)] * 2
        + [pltpu.VMEM((tokens, wide), BF16)] * 2
        + [pltpu.VMEM((1, wide), F32)] * 4
        + [pltpu.SemaphoreType.DMA((groups,))] * 3,
        compiler_params=params(51),
        cost_estimate=cost(16 * rows * inner * tokens, 9 << 20),
        name="attend",
    )(used, queries, key_lanes, value_logs, value_inverse, first_keys, first_values, key_codes[0], values_t)
    parts = swapped(parts)

    output_blocks = over_rep(output_weight)
    sent = pl.pallas_call(
        output_kernel,
        out_shape=jax.ShapeDtypeStruct((segs, rows, own), BF16),
        in_specs=[SMEM] + [VMEM] * 5,
        out_specs=VMEM,
        compiler_params=params(16),
        cost_estimate=cost(2 * rows * inner * own, 2 << 20),
        name="output",
    )(rep, parts, *output_blocks)
    return pl.pallas_call(
        sum_kernel,
        out_shape=jax.ShapeDtypeStruct((rows, own), BF16),
        in_specs=[VMEM],
        out_specs=VMEM,
        compiler_params=params(8),
        name="gather_sum",
    )(swapped(sent, LAST))


def solution(mesh):
    placed = (
        P("rep", "seg"),
        P(),
        P("rep", "seg"),
        P("rep", "seg", None),
        P("rep", "seg", None),
        P("rep", "seg", None),
        P("rep", "seg", None),
        P("rep"),
        P("seg", "rep"),
    )
    return jax.shard_map(
        sublayer, mesh=mesh, in_specs=placed, out_specs=P("rep", "seg"), check_vma=False
    )
```

profile of v0, /device:TPU:0, one launch (start us, length us, event | category | flops | bytes accessed | tf_op | source)
XLA Modules:
  0.0 82.3 jit_solution(101409334598626717)
XLA Ops:
  0.0 3.3 %collective-permute-start.1 = (bf16[1024,128]{1,0:T(8,128)(2,1)}, bf16[1024,128]{1,0:T(8,128)(2,1)S(1)}, u32[]{:S(2)}, u32[]{:S(2)}) collective-permute-start(bf16[1024,128]{1,0:T(8,128)(2,1)} %own_ref.1), channel_id=1, source_target_pairs={{0,2},{1,3},{2,0},{3,1},{4,6},{5,7},{6,4},{7,5},{8,10},{9,11},{10,... | collective-permute-start | bytes 786440 | tf_op jit(solution)/shard_map/ppermute | solution.py:301
  3.3 1.6 %broadcast_in_dim.15 = bf16[32,64,128]{2,1,0:T(8,128)(2,1)} broadcast(bf16[64,128]{1,0:T(8,128)(2,1)} %param.9), dimensions={1,2} | broadcast | bytes 540672 | tf_op jit(solution)/shard_map/broadcast_in_dim | solution.py:338
  4.9 10.1 %all-to-all-start = ((bf16[32,64,128]{2,1,0:T(8,128)(2,1)}), bf16[32,64,128]{2,1,0:T(8,128)(2,1)S(1)}, u32[]{:S(2)}, u32[]{:S(2)}) async-start(bf16[32,64,128]{2,1,0:T(8,128)(2,1)} %broadcast_in_dim.15), calls=%async_computation | async-start | bytes 1048576 | tf_op jit(solution)/shard_map/all_to_all | solution.py:309
  15.1 0.1 collective-permute-start
  15.2 0.0 collective-permute-done.1.refs_2_
  15.2 0.5 collective-permute-start.2
  15.7 0.7 divide_bitcast_fusion
  16.4 0.1 broadcast_in_dim.17
  16.5 0.1 reshape.25.lvs_ref
  16.6 0.1 broadcast_in_dim.18
  16.7 0.1 reshape.26.ivs_ref
  16.8 0.7 multiply_bitcast_fusion.1
  17.5 0.1 broadcast_in_dim.16
  17.6 0.1 reshape.24.ks_ref
  17.7 0.0 copy-start.1
  17.7 0.9 %copy-done.1 = bf16[1024,128]{1,0:T(8,128)(2,1)S(1)} copy-done((bf16[1024,128]{1,0:T(8,128)(2,1)S(1)}, bf16[1024,128]{1,0:T(8,128)(2,1)}, u32[]{:S(2)}) %copy-start.1) | copy-done | bytes 262168
  18.6 0.0 copy-start.2
  18.6 0.7 copy-done.2
  19.4 2.7 %all-to-all-done.x_ref = bf16[32,64,128]{2,1,0:T(8,128)(2,1)S(1)} async-done(((bf16[32,64,128]{2,1,0:T(8,128)(2,1)}), bf16[32,64,128]{2,1,0:T(8,128)(2,1)S(1)}, u32[]{:S(2)}, u32[]{:S(2)}) %all-to-all-start) | async-done | bytes 524320 | tf_op jit(solution)/shard_map/all_to_all | solution.py:309
  22.1 0.0 collective-permute-done.refs_1_
  22.1 0.0 collective-permute-done.2.refs_3_
  22.1 1.3 %query.1 = bf16[32,64,128]{2,1,0:T(8,128)(2,1)} custom-call(s32[1]{0:T(128)} %bitcast.rep_ref, bf16[32,64,128]{2,1,0:T(8,128)(2,1)S(1)} %all-to-all-done.x_ref, f32[32,128]{1,0:T(8,128)S(1)} %get-tuple-element.15.gain_ref, bf16[1024,128]{1,0:T(8,128)(2,1)S(1)} %get-tuple-element.16.refs_0_, bf16[1024,128]{1,0:T(8,128)(2,1)S(1)} %collective-permute-done.refs_1_, ...), custom_call_target="tpu_custom_call" | custom-call | flops 67108864 | bytes 2097152 | tf_op jit(solution)/shard_map/query/pallas_call | solution.py:390
  23.4 8.2 %all-to-all-start.1 = ((bf16[32,64,128]{2,1,0:T(8,128)(2,1)}), bf16[32,64,128]{2,1,0:T(8,128)(2,1)S(1)}, u32[]{:S(2)}, u32[]{:S(2)}) async-start(bf16[32,64,128]{2,1,0:T(8,128)(2,1)} %query.1), calls=%async_computation.1 | async-start | bytes 1048576 | tf_op jit(solution)/shard_map/all_to_all | solution.py:309
  32.3 5.7 %turn.1 = (bf16[16,2,128,512]{3,2,1,0:T(8,128)(2,1)}, bf16[4,512,256]{2,1,0:T(8,128)(2,1)S(1)}, bf16[2,2,144,512]{3,2,1,0:T(8,128)(2,1)S(1)}) custom-call(bf16[512,4096]{1,0:T(8,128)(2,1)} %bitcast.14, bf16[512,4096]{1,0:T(8,128)(2,1)} %bitcast.12), custom_call_target="tpu_custom_call" | custom-call | flops 2147483648 | bytes 8388608 | tf_op jit(solution)/shard_map/turn/pallas_call | solution.py:363
  38.0 0.2 all-to-all-done.1.q_ref
  38.2 0.0 copy-start
  38.2 5.8 %attend.1 = bf16[32,72,128]{2,1,0:T(8,128)(2,1)} custom-call(s32[1]{0:T(128)S(6)} %min.6.used_ref, bf16[32,64,128]{2,1,0:T(8,128)(2,1)S(1)} %all-to-all-done.1.q_ref, f32[4,4096]{1,0:T(4,128)S(1)} %reshape.24.ks_ref, f32[4,4096]{1,0:T(4,128)S(1)} %reshape.25.lvs_ref, f32[4,4096]{1,0:T(4,128)S(1)} %reshape.26.ivs_ref, ...), custom_call_target="tpu_custom_call" | custom-call | flops 2147483648 | bytes 9437184 | tf_op jit(solution)/shard_map/attend/pallas_call | solution.py:393
  44.0 7.5 %all-to-all-start.2 = ((bf16[32,72,128]{2,1,0:T(8,128)(2,1)}), bf16[32,72,128]{2,1,0:T(8,128)(2,1)S(1)}, u32[]{:S(2)}, u32[]{:S(2)}) async-start(bf16[32,72,128]{2,1,0:T(8,128)(2,1)} %attend.1), calls=%async_computation.2 | async-start | bytes 1179648 | tf_op jit(solution)/shard_map/all_to_all | solution.py:309
  51.5 0.0 copy-done
  51.5 2.4 %collective-permute-start.4 = (bf16[128,1024]{1,0:T(8,128)(2,1)S(1)}, bf16[128,1024]{1,0:T(8,128)(2,1)S(1)}, u32[]{:S(2)}, u32[]{:S(2)}) collective-permute-start(bf16[128,1024]{1,0:T(8,128)(2,1)S(1)} %copy-done), channel_id=1, source_target_pairs={{0,2},{1,3},{2,0},{3,1},{4,6},{5,7},{6,4},{7,5},{8,10},{9,11},{10,... | collective-permute-start | bytes 786440 | tf_op jit(solution)/shard_map/ppermute | solution.py:301
  53.9 0.0 collective-permute-start.3
  53.9 10.9 %collective-permute-done.4.refs_2_ = bf16[128,1024]{1,0:T(8,128)(2,1)S(1)} collective-permute-done((bf16[128,1024]{1,0:T(8,128)(2,1)S(1)}, bf16[128,1024]{1,0:T(8,128)(2,1)S(1)}, u32[]{:S(2)}, u32[]{:S(2)}) %collective-permute-start.4) | collective-permute-done | bytes 262176 | tf_op jit(solution)/shard_map/ppermute | solution.py:301
  64.8 0.0 collective-permute-start.5
  64.8 0.0 collective-permute-done.3.refs_1_
  64.8 1.5 %collective-permute-done.5.refs_3_ = bf16[128,1024]{1,0:T(8,128)(2,1)S(1)} collective-permute-done((bf16[128,1024]{1,0:T(8,128)(2,1)S(1)}, bf16[128,1024]{1,0:T(8,128)(2,1)S(1)}, u32[]{:S(2)}, u32[]{:S(2)}) %collective-permute-start.5) | collective-permute-done | bytes 262176 | tf_op jit(solution)/shard_map/ppermute | solution.py:303
  66.4 0.0 all-to-all-done.2.part_ref
  66.4 0.5 output.1
  66.9 14.7 %all_to_all.20.part_ref = bf16[32,64,128]{2,1,0:T(8,128)(2,1)S(1)} all-to-all(bf16[32,64,128]{2,1,0:T(8,128)(2,1)S(1)} %output.1), channel_id=1, replica_groups={{104,108,96,100,120,124,112,116,72,76,64,68,88,92,80,84,40,44,32,36,56,..., dimensions={0} | all-to-all | bytes 1048576 | tf_op jit(solution)/shard_map/all_to_all | solution.py:309
  81.6 0.7 gather_sum.1
  (1 shorter events, 0.0 us)
Async XLA Ops:
  0.0 15.2 %collective-permute-start.1 = (bf16[1024,128]{1,0:T(8,128)(2,1)}, bf16[1024,128]{1,0:T(8,128)(2,1)S(1)}, u32[]{:S(2)}, u32[]{:S(2)}) collective-permute-start(bf16[1024,128]{1,0:T(8,128)(2,1)} %own_ref.1), channel_id=1, source_target_pairs={{0,2},{1,3},{2,0},{3,1},{4,6},{5,7},{6,4},{7,5},{8,10},{9,11},{10,... | collective-permute-start | bytes 786440 | tf_op jit(solution)/shard_map/ppermute | solution.py:301
  4.9 17.1 %all-to-all-start = ((bf16[32,64,128]{2,1,0:T(8,128)(2,1)}), bf16[32,64,128]{2,1,0:T(8,128)(2,1)S(1)}, u32[]{:S(2)}, u32[]{:S(2)}) async-start(bf16[32,64,128]{2,1,0:T(8,128)(2,1)} %broadcast_in_dim.15), calls=%async_computation | async-start | bytes 1048576 | tf_op jit(solution)/shard_map/all_to_all | solution.py:309
  15.1 7.0 %collective-permute-start = (bf16[1024,128]{1,0:T(8,128)(2,1)}, bf16[1024,128]{1,0:T(8,128)(2,1)S(1)}, u32[]{:S(2)}, u32[]{:S(2)}) collective-permute-start(bf16[1024,128]{1,0:T(8,128)(2,1)} %own_ref.1), channel_id=1, source_target_pairs={{0,1},{1,0},{2,3},{3,2},{4,5},{5,4},{6,7},{7,6},{8,9},{9,8},{10,11... | collective-permute-start | bytes 786440 | tf_op jit(solution)/shard_map/ppermute | solution.py:302
  15.2 6.9 %collective-permute-start.2 = (bf16[1024,128]{1,0:T(8,128)(2,1)S(1)}, bf16[1024,128]{1,0:T(8,128)(2,1)S(1)}, u32[]{:S(2)}, u32[]{:S(2)}) collective-permute-start(bf16[1024,128]{1,0:T(8,128)(2,1)S(1)} %collective-permute-done.1.refs_2_), channel_id=1, source_target_pairs={{0,1},{1,0},{2,3},{3,2},{4,5},{5,4},{6,7},{7,6},{8,9},{9,8},{10,11... | collective-permute-start | bytes 786440 | tf_op jit(solution)/shard_map/ppermute | solution.py:303
  17.7 1.0 %copy-start.1 = (bf16[1024,128]{1,0:T(8,128)(2,1)S(1)}, bf16[1024,128]{1,0:T(8,128)(2,1)}, u32[]{:S(2)}) copy-start(bf16[1024,128]{1,0:T(8,128)(2,1)} %own_ref.1) | copy-start | bytes 786436
  18.6 0.7 copy-start.2
  23.4 14.8 %all-to-all-start.1 = ((bf16[32,64,128]{2,1,0:T(8,128)(2,1)}), bf16[32,64,128]{2,1,0:T(8,128)(2,1)S(1)}, u32[]{:S(2)}, u32[]{:S(2)}) async-start(bf16[32,64,128]{2,1,0:T(8,128)(2,1)} %query.1), calls=%async_computation.1 | async-start | bytes 1048576 | tf_op jit(solution)/shard_map/all_to_all | solution.py:309
  38.2 13.3 %copy-start = (bf16[128,1024]{1,0:T(8,128)(2,1)S(1)}, bf16[128,1024]{1,0:T(8,128)(2,1)}, u32[]{:S(2)}) copy-start(bf16[128,1024]{1,0:T(8,128)(2,1)} %refs_0_.1) | copy-start | bytes 786436
  44.0 22.4 %all-to-all-start.2 = ((bf16[32,72,128]{2,1,0:T(8,128)(2,1)}), bf16[32,72,128]{2,1,0:T(8,128)(2,1)S(1)}, u32[]{:S(2)}, u32[]{:S(2)}) async-start(bf16[32,72,128]{2,1,0:T(8,128)(2,1)} %attend.1), calls=%async_computation.2 | async-start | bytes 1179648 | tf_op jit(solution)/shard_map/all_to_all | solution.py:309
  51.5 13.3 %collective-permute-start.4 = (bf16[128,1024]{1,0:T(8,128)(2,1)S(1)}, bf16[128,1024]{1,0:T(8,128)(2,1)S(1)}, u32[]{:S(2)}, u32[]{:S(2)}) collective-permute-start(bf16[128,1024]{1,0:T(8,128)(2,1)S(1)} %copy-done), channel_id=1, source_target_pairs={{0,2},{1,3},{2,0},{3,1},{4,6},{5,7},{6,4},{7,5},{8,10},{9,11},{10,... | collective-permute-start | bytes 786440 | tf_op jit(solution)/shard_map/ppermute | solution.py:301
  53.9 10.9 %collective-permute-start.3 = (bf16[128,1024]{1,0:T(8,128)(2,1)S(1)}, bf16[128,1024]{1,0:T(8,128)(2,1)S(1)}, u32[]{:S(2)}, u32[]{:S(2)}) collective-permute-start(bf16[128,1024]{1,0:T(8,128)(2,1)S(1)} %copy-done), channel_id=1, source_target_pairs={{0,1},{1,0},{2,3},{3,2},{4,5},{5,4},{6,7},{7,6},{8,9},{9,8},{10,11... | collective-permute-start | bytes 786440 | tf_op jit(solution)/shard_map/ppermute | solution.py:302
  64.8 1.5 %collective-permute-start.5 = (bf16[128,1024]{1,0:T(8,128)(2,1)S(1)}, bf16[128,1024]{1,0:T(8,128)(2,1)S(1)}, u32[]{:S(2)}, u32[]{:S(2)}) collective-permute-start(bf16[128,1024]{1,0:T(8,128)(2,1)S(1)} %collective-permute-done.4.refs_2_), channel_id=1, source_target_pairs={{0,1},{1,0},{2,3},{3,2},{4,5},{5,4},{6,7},{7,6},{8,9},{9,8},{10,11... | collective-permute-start | bytes 786440 | tf_op jit(solution)/shard_map/ppermute | solution.py:303
where the time goes:
time: 83 us; the launch traced here: 82.3 us
  starting transfers between devices  32.2 us (39%)
  waiting for transfers between devices  15.3 us (18%)
  blocking collectives  14.7 us (18%)
  Pallas kernels  14.1 us (17%)
  local copies, waits for them, and re-layouts  3.89 us (5%)
  other arithmetic  1.37 us (2%)
    all_to_all x3, starting transfers between devices, swapped(): lax.all_to_all(blocks, 'seg', split_axis=0, concat_axis=0, tiled=True, ax...  25.9 us
    all_to_all x1, blocking collectives, swapped(): lax.all_to_all(blocks, 'seg', split_axis=0, concat_axis=0, tiled=True, ax...  14.7 us
    ppermute x2, waiting for transfers between devices, over_rep(): far = lax.ppermute(block, 'rep', CHIP)  10.9 us
    pallas_call x1, Pallas kernels, sublayer(): pl.pallas_call(attend_kernel, out_shape=jax.ShapeDtypeStruct((segs, head_...  5.81 us
    ppermute x2, starting transfers between devices, over_rep(): far = lax.ppermute(block, 'rep', CHIP)  5.72 us
    pallas_call x1, Pallas kernels, sublayer(): values_t, first_keys, first_values = turn_call(value_codes[0], key_codes[0])  5.68 us
    all_to_all x3, waiting for transfers between devices, swapped(): lax.all_to_all(blocks, 'seg', split_axis=0, concat_axis=0, tiled=True, ax...  2.89 us
    unnamed x6, local copies, waits for them, and re-layouts  1.67 us
  transfers between devices with their start and end apart: 9, of which 4 were waited for; matrix products, arithmetic and copies ran while one was open for 4% of the time, Pallas kernels for 7%

commit v1 on v0

--- a/solution.py
+++ b/solution.py
@@ -13,8 +13,7 @@
 STAT_ROWS = 8
 SUM_ROWS = 16
 EMPTY = -1e30
-FIRST = 10
-LAST = 26
+FIRST = 26
 VMEM = pl.BlockSpec(memory_space=pltpu.VMEM)
 SMEM = pl.BlockSpec(memory_space=pltpu.SMEM)
 HBM = pl.BlockSpec(memory_space=pltpu.HBM)
@@ -68,27 +67,22 @@
     gain_out[...] = gain_ref[...]
 
 
-def picks_of(tokens):
+def turn_kernel(v_ref, k_ref, out_ref, k_first, vt_first):
+    tokens = v_ref.shape[0]
     row = lax.broadcasted_iota(jnp.int32, (SUM_ROWS, tokens), 0)
     block = lax.broadcasted_iota(jnp.int32, (SUM_ROWS, tokens), 1) // LANES
-    return jnp.where(row == block, 1.0, 0.0).astype(BF16)
-
-
-def turn_kernel(v_ref, k_ref, out_ref, k_first, vt_first):
+    picks = jnp.where(row == block, 1.0, 0.0).astype(BF16)
     for j in range(out_ref.shape[0]):
         for i in range(2):
             at = slice((2 * j + i) * LANES, (2 * j + i + 1) * LANES)
-            out_ref[j, i] = v_ref[:, at].T
+            out_ref[j, i, 0:LANES, :] = v_ref[:, at].T
+            out_ref[j, i, LANES : LANES + SUM_ROWS, :] = picks
 
     @pl.when(pl.program_id(0) == 0)
     def _():
         for g in range(k_first.shape[0]):
             k_first[g] = k_ref[:, 2 * g * LANES : 2 * (g + 1) * LANES]
-        picks = picks_of(v_ref.shape[0])
-        for j in range(vt_first.shape[0]):
-            for i in range(2):
-                vt_first[j, i, 0:LANES, :] = out_ref[j, i]
-                vt_first[j, i, LANES : LANES + SUM_ROWS, :] = picks
+        vt_first[...] = out_ref[0 : vt_first.shape[0]]
 
 
 def attend_kernel(
@@ -110,9 +104,7 @@
         return pltpu.make_async_copy(k_hbm.at[:, lanes_of(g)], k_buf.at[g], k_sems.at[g])
 
     def vt_copy(g):
-        return pltpu.make_async_copy(
-            vt_hbm.at[g], vt_buf.at[g, :, pl.ds(0, LANES), :], vt_sems.at[g]
-        )
+        return pltpu.make_async_copy(vt_hbm.at[g], vt_buf.at[g], vt_sems.at[g])
 
     def out_copy(g):
         at = pl.ds((2 * g) ^ FIRST, 2)
@@ -128,11 +120,6 @@
 
     for i in range(2, groups // 2 + 1):
         fetch(i)
-
-    picks = picks_of(k_buf.shape[1])
-    for g in range(vt_early, groups):
-        for i in range(2):
-            vt_buf[g, i, LANES : LANES + SUM_ROWS, :] = picks
 
     def put(pair, sums, log_sum):
         out_ref[pair ^ FIRST, 0:half, :] = sums.astype(BF16)
@@ -283,7 +270,7 @@
         first = (rep_ref[0] ^ i) * each
         update = jnp.dot(attended, w_ref[...], preferred_element_type=F32)
         for j in range(each):
-            out_ref[(first + j) ^ LAST] = update[:, j * LANES : (j + 1) * LANES].astype(BF16)
+            out_ref[(first + j) ^ FIRST] = update[:, j * LANES : (j + 1) * LANES].astype(BF16)
 
 
 def sum_kernel(part_ref, out_ref):
@@ -304,8 +291,8 @@
     return block, near, far, both
 
 
-def swapped(blocks, lead=FIRST):
-    order = [[j ^ lead for j in range(blocks.shape[0])]]
+def swapped(blocks):
+    order = [[j ^ FIRST for j in range(blocks.shape[0])]]
     return lax.all_to_all(
         blocks, "seg", split_axis=0, concat_axis=0, tiled=True, axis_index_groups=order
     )
@@ -343,7 +330,7 @@
         turn_kernel,
         grid=(steps,),
         out_shape=(
-            jax.ShapeDtypeStruct((groups, 2, LANES, tokens), BF16),
+            jax.ShapeDtypeStruct((groups, 2, height, tokens), BF16),
             jax.ShapeDtypeStruct((4, tokens, wide), BF16),
             jax.ShapeDtypeStruct((2, 2, height, tokens), BF16),
         ),
@@ -352,7 +339,7 @@
             pl.BlockSpec((tokens, 4 * wide), lambda i: (0, 0)),
         ],
         out_specs=(
-            pl.BlockSpec((groups // steps, 2, LANES, tokens), lambda i: (i, 0, 0, 0)),
+            pl.BlockSpec((groups // steps, 2, height, tokens), lambda i: (i, 0, 0, 0)),
             pl.BlockSpec((4, tokens, wide), lambda i: (0, 0, 0)),
             pl.BlockSpec((2, 2, height, tokens), lambda i: (0, 0, 0, 0)),
         ),
@@ -427,7 +414,7 @@
         out_specs=VMEM,
         compiler_params=params(8),
         name="gather_sum",
-    )(swapped(sent, LAST))
+    )(swapped(sent))
 
 
 def solution(mesh):

time: 83 us -> 83.2 us (level)
  starting transfers between devices: 32.2 us -> 33.6 us
  waiting for transfers between devices: 15.3 us -> 14 us
    all_to_all x3, starting transfers between devices: 25.9 us -> 28.4 us  [swapped(): lax.all_to_all(blocks, 'seg', split_axis=0, concat_axis=0, tiled=True, ax...]
    all_to_all x3, waiting for transfers between devices: 2.89 us -> 1.71 us  [swapped(): lax.all_to_all(blocks, 'seg', split_axis=0, concat_axis=0, tiled=True, ax...]
    ppermute x2, starting transfers between devices: 5.72 us -> 4.7 us  [over_rep(): far = lax.ppermute(block, 'rep', CHIP)]
  transfers between devices with their start and end apart: 9 -> 9, of which waited for: 4 -> 3; matrix products, arithmetic and copies ran while one was open for 4% -> 4% of each run, Pallas kernels for 7% -> 7%
where the time goes in v1:
time: 83.2 us; the launch traced here: 82.6 us
  starting transfers between devices  33.6 us (40%)
  blocking collectives  14.7 us (18%)
  Pallas kernels  14.1 us (17%)
  waiting for transfers between devices  14 us (17%)
  local copies, waits for them, and re-layouts  3.89 us (5%)
  other arithmetic  1.37 us (2%)
    all_to_all x3, starting transfers between devices, swapped(): lax.all_to_all(blocks, 'seg', split_axis=0, concat_axis=0, tiled=True, ax...  28.4 us
    all_to_all x1, blocking collectives, swapped(): lax.all_to_all(blocks, 'seg', split_axis=0, concat_axis=0, tiled=True, ax...  14.7 us
    ppermute x2, waiting for transfers between devices, over_rep(): far = lax.ppermute(block, 'rep', CHIP)  10.8 us
    pallas_call x1, Pallas kernels, sublayer(): values_t, first_keys, first_values = turn_call(value_codes[0], key_codes[0])  5.79 us
    pallas_call x1, Pallas kernels, sublayer(): pl.pallas_call(attend_kernel, out_shape=jax.ShapeDtypeStruct((segs, head_...  5.76 us
    ppermute x2, starting transfers between devices, over_rep(): far = lax.ppermute(block, 'rep', CHIP)  4.7 us
    all_to_all x3, waiting for transfers between devices, swapped(): lax.all_to_all(blocks, 'seg', split_axis=0, concat_axis=0, tiled=True, ax...  1.71 us
    unnamed x6, local copies, waits for them, and re-layouts  1.67 us
  transfers between devices with their start and end apart: 9, of which 3 were waited for; matrix products, arithmetic and copies ran while one was open for 4% of the time, Pallas kernels for 7%

profile of v1, /device:TPU:0, one launch (start us, length us, event | category | flops | bytes accessed | tf_op | source)
XLA Modules:
  0.0 82.6 jit_solution(16818271106540397025)
XLA Ops:
  0.0 3.3 %collective-permute-start.1 = (bf16[1024,128]{1,0:T(8,128)(2,1)}, bf16[1024,128]{1,0:T(8,128)(2,1)S(1)}, u32[]{:S(2)}, u32[]{:S(2)}) collective-permute-start(bf16[1024,128]{1,0:T(8,128)(2,1)} %own_ref.1), channel_id=1, source_target_pairs={{0,2},{1,3},{2,0},{3,1},{4,6},{5,7},{6,4},{7,5},{8,10},{9,11},{10,... | collective-permute-start | bytes 786440 | tf_op jit(solution)/shard_map/ppermute | solution.py:288
  3.3 1.6 %broadcast_in_dim.15 = bf16[32,64,128]{2,1,0:T(8,128)(2,1)} broadcast(bf16[64,128]{1,0:T(8,128)(2,1)} %param.9), dimensions={1,2} | broadcast | bytes 540672 | tf_op jit(solution)/shard_map/broadcast_in_dim | solution.py:325
  4.9 11.0 %all-to-all-start = ((bf16[32,64,128]{2,1,0:T(8,128)(2,1)}), bf16[32,64,128]{2,1,0:T(8,128)(2,1)S(1)}, u32[]{:S(2)}, u32[]{:S(2)}) async-start(bf16[32,64,128]{2,1,0:T(8,128)(2,1)} %broadcast_in_dim.15), calls=%async_computation | async-start | bytes 1048576 | tf_op jit(solution)/shard_map/all_to_all | solution.py:296
  15.9 0.1 collective-permute-start
  16.0 0.0 collective-permute-done.1.refs_2_
  16.0 0.5 collective-permute-start.2
  16.5 0.7 divide_bitcast_fusion
  17.2 0.1 broadcast_in_dim.17
  17.3 0.1 reshape.25.lvs_ref
  17.4 0.1 broadcast_in_dim.18
  17.5 0.1 reshape.26.ivs_ref
  17.6 0.7 multiply_bitcast_fusion.1
  18.3 0.1 broadcast_in_dim.16
  18.4 0.1 reshape.24.ks_ref
  18.5 0.0 copy-start.1
  18.5 0.9 %copy-done.1 = bf16[1024,128]{1,0:T(8,128)(2,1)S(1)} copy-done((bf16[1024,128]{1,0:T(8,128)(2,1)S(1)}, bf16[1024,128]{1,0:T(8,128)(2,1)}, u32[]{:S(2)}) %copy-start.1) | copy-done | bytes 262168
  19.5 0.0 copy-start.2
  19.5 0.7 copy-done.2
  20.2 1.7 %all-to-all-done.x_ref = bf16[32,64,128]{2,1,0:T(8,128)(2,1)S(1)} async-done(((bf16[32,64,128]{2,1,0:T(8,128)(2,1)}), bf16[32,64,128]{2,1,0:T(8,128)(2,1)S(1)}, u32[]{:S(2)}, u32[]{:S(2)}) %all-to-all-start) | async-done | bytes 524320 | tf_op jit(solution)/shard_map/all_to_all | solution.py:296
  21.9 0.0 collective-permute-done.refs_1_
  21.9 0.0 collective-permute-done.2.refs_3_
  21.9 1.4 %query.1 = bf16[32,64,128]{2,1,0:T(8,128)(2,1)} custom-call(s32[1]{0:T(128)} %bitcast.rep_ref, bf16[32,64,128]{2,1,0:T(8,128)(2,1)S(1)} %all-to-all-done.x_ref, f32[32,128]{1,0:T(8,128)S(1)} %get-tuple-element.15.gain_ref, bf16[1024,128]{1,0:T(8,128)(2,1)S(1)} %get-tuple-element.16.refs_0_, bf16[1024,128]{1,0:T(8,128)(2,1)S(1)} %collective-permute-done.refs_1_, ...), custom_call_target="tpu_custom_call" | custom-call | flops 67108864 | bytes 2097152 | tf_op jit(solution)/shard_map/query/pallas_call | solution.py:377
  23.3 9.1 %all-to-all-start.1 = ((bf16[32,64,128]{2,1,0:T(8,128)(2,1)}), bf16[32,64,128]{2,1,0:T(8,128)(2,1)S(1)}, u32[]{:S(2)}, u32[]{:S(2)}) async-start(bf16[32,64,128]{2,1,0:T(8,128)(2,1)} %query.1), calls=%async_computation.1 | async-start | bytes 1048576 | tf_op jit(solution)/shard_map/all_to_all | solution.py:296
  33.0 5.8 %turn.1 = (bf16[16,2,144,512]{3,2,1,0:T(8,128)(2,1)}, bf16[4,512,256]{2,1,0:T(8,128)(2,1)S(1)}, bf16[2,2,144,512]{3,2,1,0:T(8,128)(2,1)S(1)}) custom-call(bf16[512,4096]{1,0:T(8,128)(2,1)} %bitcast.14, bf16[512,4096]{1,0:T(8,128)(2,1)} %bitcast.12), custom_call_target="tpu_custom_call" | custom-call | flops 2147483648 | bytes 8388608 | tf_op jit(solution)/shard_map/turn/pallas_call | solution.py:350
  38.8 0.0 all-to-all-done.1.q_ref
  38.8 0.0 copy-start
  38.8 5.8 %attend.1 = bf16[32,72,128]{2,1,0:T(8,128)(2,1)} custom-call(s32[1]{0:T(128)S(6)} %min.6.used_ref, bf16[32,64,128]{2,1,0:T(8,128)(2,1)S(1)} %all-to-all-done.1.q_ref, f32[4,4096]{1,0:T(4,128)S(1)} %reshape.24.ks_ref, f32[4,4096]{1,0:T(4,128)S(1)} %reshape.25.lvs_ref, f32[4,4096]{1,0:T(4,128)S(1)} %reshape.26.ivs_ref, ...), custom_call_target="tpu_custom_call" | custom-call | flops 2147483648 | bytes 9437184 | tf_op jit(solution)/shard_map/attend/pallas_call | solution.py:380
  44.6 8.3 %all-to-all-start.2 = ((bf16[32,72,128]{2,1,0:T(8,128)(2,1)}), bf16[32,72,128]{2,1,0:T(8,128)(2,1)S(1)}, u32[]{:S(2)}, u32[]{:S(2)}) async-start(bf16[32,72,128]{2,1,0:T(8,128)(2,1)} %attend.1), calls=%async_computation.2 | async-start | bytes 1179648 | tf_op jit(solution)/shard_map/all_to_all | solution.py:296
  52.9 0.0 copy-done
  52.9 1.4 %collective-permute-start.4 = (bf16[128,1024]{1,0:T(8,128)(2,1)S(1)}, bf16[128,1024]{1,0:T(8,128)(2,1)S(1)}, u32[]{:S(2)}, u32[]{:S(2)}) collective-permute-start(bf16[128,1024]{1,0:T(8,128)(2,1)S(1)} %copy-done), channel_id=1, source_target_pairs={{0,2},{1,3},{2,0},{3,1},{4,6},{5,7},{6,4},{7,5},{8,10},{9,11},{10,... | collective-permute-start | bytes 786440 | tf_op jit(solution)/shard_map/ppermute | solution.py:288
  54.3 0.0 collective-permute-start.3
  54.3 10.8 %collective-permute-done.4.refs_2_ = bf16[128,1024]{1,0:T(8,128)(2,1)S(1)} collective-permute-done((bf16[128,1024]{1,0:T(8,128)(2,1)S(1)}, bf16[128,1024]{1,0:T(8,128)(2,1)S(1)}, u32[]{:S(2)}, u32[]{:S(2)}) %collective-permute-start.4) | collective-permute-done | bytes 262176 | tf_op jit(solution)/shard_map/ppermute | solution.py:288
  65.1 0.0 collective-permute-start.5
  65.1 0.0 collective-permute-done.3.refs_1_
  65.1 1.5 %collective-permute-done.5.refs_3_ = bf16[128,1024]{1,0:T(8,128)(2,1)S(1)} collective-permute-done((bf16[128,1024]{1,0:T(8,128)(2,1)S(1)}, bf16[128,1024]{1,0:T(8,128)(2,1)S(1)}, u32[]{:S(2)}, u32[]{:S(2)}) %collective-permute-start.5) | collective-permute-done | bytes 262176 | tf_op jit(solution)/shard_map/ppermute | solution.py:290
  66.6 0.0 all-to-all-done.2.part_ref
  66.6 0.5 output.1
  67.2 14.7 %all_to_all.20.part_ref = bf16[32,64,128]{2,1,0:T(8,128)(2,1)S(1)} all-to-all(bf16[32,64,128]{2,1,0:T(8,128)(2,1)S(1)} %output.1), channel_id=1, replica_groups={{104,108,96,100,120,124,112,116,72,76,64,68,88,92,80,84,40,44,32,36,56,..., dimensions={0} | all-to-all | bytes 1048576 | tf_op jit(solution)/shard_map/all_to_all | solution.py:296
  81.9 0.7 gather_sum.1
  (1 shorter events, 0.0 us)
Async XLA Ops:
  0.0 16.0 %collective-permute-start.1 = (bf16[1024,128]{1,0:T(8,128)(2,1)}, bf16[1024,128]{1,0:T(8,128)(2,1)S(1)}, u32[]{:S(2)}, u32[]{:S(2)}) collective-permute-start(bf16[1024,128]{1,0:T(8,128)(2,1)} %own_ref.1), channel_id=1, source_target_pairs={{0,2},{1,3},{2,0},{3,1},{4,6},{5,7},{6,4},{7,5},{8,10},{9,11},{10,... | collective-permute-start | bytes 786440 | tf_op jit(solution)/shard_map/ppermute | solution.py:288
  4.9 17.0 %all-to-all-start = ((bf16[32,64,128]{2,1,0:T(8,128)(2,1)}), bf16[32,64,128]{2,1,0:T(8,128)(2,1)S(1)}, u32[]{:S(2)}, u32[]{:S(2)}) async-start(bf16[32,64,128]{2,1,0:T(8,128)(2,1)} %broadcast_in_dim.15), calls=%async_computation | async-start | bytes 1048576 | tf_op jit(solution)/shard_map/all_to_all | solution.py:296
  15.9 6.0 %collective-permute-start = (bf16[1024,128]{1,0:T(8,128)(2,1)}, bf16[1024,128]{1,0:T(8,128)(2,1)S(1)}, u32[]{:S(2)}, u32[]{:S(2)}) collective-permute-start(bf16[1024,128]{1,0:T(8,128)(2,1)} %own_ref.1), channel_id=1, source_target_pairs={{0,1},{1,0},{2,3},{3,2},{4,5},{5,4},{6,7},{7,6},{8,9},{9,8},{10,11... | collective-permute-start | bytes 786440 | tf_op jit(solution)/shard_map/ppermute | solution.py:289
  16.0 5.9 %collective-permute-start.2 = (bf16[1024,128]{1,0:T(8,128)(2,1)S(1)}, bf16[1024,128]{1,0:T(8,128)(2,1)S(1)}, u32[]{:S(2)}, u32[]{:S(2)}) collective-permute-start(bf16[1024,128]{1,0:T(8,128)(2,1)S(1)} %collective-permute-done.1.refs_2_), channel_id=1, source_target_pairs={{0,1},{1,0},{2,3},{3,2},{4,5},{5,4},{6,7},{7,6},{8,9},{9,8},{10,11... | collective-permute-start | bytes 786440 | tf_op jit(solution)/shard_map/ppermute | solution.py:290
  18.5 1.0 %copy-start.1 = (bf16[1024,128]{1,0:T(8,128)(2,1)S(1)}, bf16[1024,128]{1,0:T(8,128)(2,1)}, u32[]{:S(2)}) copy-start(bf16[1024,128]{1,0:T(8,128)(2,1)} %own_ref.1) | copy-start | bytes 786436
  19.5 0.7 copy-start.2
  23.3 15.5 %all-to-all-start.1 = ((bf16[32,64,128]{2,1,0:T(8,128)(2,1)}), bf16[32,64,128]{2,1,0:T(8,128)(2,1)S(1)}, u32[]{:S(2)}, u32[]{:S(2)}) async-start(bf16[32,64,128]{2,1,0:T(8,128)(2,1)} %query.1), calls=%async_computation.1 | async-start | bytes 1048576 | tf_op jit(solution)/shard_map/all_to_all | solution.py:296
  38.8 14.1 %copy-start = (bf16[128,1024]{1,0:T(8,128)(2,1)S(1)}, bf16[128,1024]{1,0:T(8,128)(2,1)}, u32[]{:S(2)}) copy-start(bf16[128,1024]{1,0:T(8,128)(2,1)} %refs_0_.1) | copy-start | bytes 786436
  44.6 22.1 %all-to-all-start.2 = ((bf16[32,72,128]{2,1,0:T(8,128)(2,1)}), bf16[32,72,128]{2,1,0:T(8,128)(2,1)S(1)}, u32[]{:S(2)}, u32[]{:S(2)}) async-start(bf16[32,72,128]{2,1,0:T(8,128)(2,1)} %attend.1), calls=%async_computation.2 | async-start | bytes 1179648 | tf_op jit(solution)/shard_map/all_to_all | solution.py:296
  52.9 12.2 %collective-permute-start.4 = (bf16[128,1024]{1,0:T(8,128)(2,1)S(1)}, bf16[128,1024]{1,0:T(8,128)(2,1)S(1)}, u32[]{:S(2)}, u32[]{:S(2)}) collective-permute-start(bf16[128,1024]{1,0:T(8,128)(2,1)S(1)} %copy-done), channel_id=1, source_target_pairs={{0,2},{1,3},{2,0},{3,1},{4,6},{5,7},{6,4},{7,5},{8,10},{9,11},{10,... | collective-permute-start | bytes 786440 | tf_op jit(solution)/shard_map/ppermute | solution.py:288
  54.3 10.8 %collective-permute-start.3 = (bf16[128,1024]{1,0:T(8,128)(2,1)S(1)}, bf16[128,1024]{1,0:T(8,128)(2,1)S(1)}, u32[]{:S(2)}, u32[]{:S(2)}) collective-permute-start(bf16[128,1024]{1,0:T(8,128)(2,1)S(1)} %copy-done), channel_id=1, source_target_pairs={{0,1},{1,0},{2,3},{3,2},{4,5},{5,4},{6,7},{7,6},{8,9},{9,8},{10,11... | collective-permute-start | bytes 786440 | tf_op jit(solution)/shard_map/ppermute | solution.py:289
  65.1 1.5 %collective-permute-start.5 = (bf16[128,1024]{1,0:T(8,128)(2,1)S(1)}, bf16[128,1024]{1,0:T(8,128)(2,1)S(1)}, u32[]{:S(2)}, u32[]{:S(2)}) collective-permute-start(bf16[128,1024]{1,0:T(8,128)(2,1)S(1)} %collective-permute-done.4.refs_2_), channel_id=1, source_target_pairs={{0,1},{1,0},{2,3},{3,2},{4,5},{5,4},{6,7},{7,6},{8,9},{9,8},{10,11... | collective-permute-start | bytes 786440 | tf_op jit(solution)/shard_map/ppermute | solution.py:290
